TPU v7x, 8 devices: a whole 2x2x1 slice. The times are simulated.
8 devices in a mesh: dp: 2 (over z, y), sp: 4 (over x, core).
Axes of the slice: x: 2, y: 2, z: 1, core: 2. Of those that a mesh axis runs over, the one named last changes fastest.
Arguments:
- hidden: bfloat16 [32, 1024, 2560], P('dp', 'sp'), parts along dimension 0
- seq_lens: int32 [32], P('dp'), parts along dimension 0
- ln1_gain: float32 [2560], replicated
- ln1_bias: float32 [2560], replicated
- ln2_gain: float32 [2560], replicated
- ln2_bias: float32 [2560], replicated
- w_qkv: bfloat16 [2560, 7680], replicated
- b_qkv: float32 [32, 3, 80], replicated
- w_out: bfloat16 [2560, 2560], replicated
- b_out: float32 [2560], replicated
- w_up: bfloat16 [2560, 10240], replicated
- b_up: float32 [10240], replicated
- w_down: bfloat16 [10240, 2560], replicated
- b_down: float32 [2560], replicated
Outputs:
- output 1: bfloat16 [32, 1024, 2560], P('dp', 'sp'), parts along dimension 0
- output 2: bfloat16 [32, 32, 1024, 80], P('dp', 'sp'), parts along dimension 0
- output 3: bfloat16 [32, 32, 1024, 80], P('dp', 'sp'), parts along dimension 0
There are 2 independent parts. A program takes and returns all parts, laid end to end along the dimension named above; an argument that names none is the same for every part.
All inputs are finite; a program needn't handle non-finite values.
Results may differ from a plain program's by a relative error of at most 0.00451203.
Values are sent between devices in bfloat16 or wider.
A program may use at most 1 GiB of HBM per device.

v0:
```python
import functools

import jax
import jax.numpy as jnp
from jax import lax
from jax.experimental import pallas as pl
from jax.experimental.pallas import tpu as pltpu
from jax.sharding import PartitionSpec as P


LN_EPS = 1e-5
ROT_BASE = 10000.0
LOG2_E = 1.4426950408889634


def rotary_tables(n_positions, head_dim):
    rot_dim = head_dim // 4
    half_rot = rot_dim // 2
    inv_freq = ROT_BASE ** (-2.0 * jnp.arange(half_rot, dtype=jnp.float32) / rot_dim)
    angles = inv_freq[:, None] * jnp.arange(n_positions).astype(jnp.float32)[None, :]
    cosines, sines = jnp.cos(angles), jnp.sin(angles)
    rest = jnp.zeros((-rot_dim % 8, n_positions), jnp.float32)
    zeros = jnp.zeros_like(sines)
    keep = jnp.concatenate([cosines, cosines, rest + 1.0], axis=0)
    below = jnp.concatenate([-sines, zeros, rest], axis=0)
    above = jnp.concatenate([zeros, sines, rest], axis=0)
    return keep, below, above


def norm_kernel(n_halves, n_prompts, x_ref, g1_ref, b1_ref, g2_ref, b2_ref, *outs):
    step = pl.program_id(0)
    rows = x_ref[0].astype(jnp.float32)
    centered = rows - jnp.mean(rows, axis=-1, keepdims=True)
    variance = jnp.mean(centered * centered, axis=-1, keepdims=True)
    normed = centered * lax.rsqrt(variance + LN_EPS)
    a_rows = (normed * g1_ref[...] + b1_ref[...]).astype(jnp.bfloat16)
    m_rows = (normed * g2_ref[...] + b2_ref[...]).astype(jnp.bfloat16)
    for parts, result in ((outs[:n_halves], a_rows), (outs[n_halves:], m_rows)):
        size = n_prompts // len(parts)
        for g, part in enumerate(parts):
            @pl.when(step // size == g)
            def _(part=part, result=result):
                part[0] = result


def part_spec(shape, start, count):
    return pl.BlockSpec((1,) + shape, lambda i, *_: (jnp.clip(i - start, 0, count - 1), 0, 0))


def norms(hidden, n_halves, n_quarters, g1, b1, g2, b2):
    n_prompts, rows, width = hidden.shape
    vec = pl.BlockSpec((1, width), lambda i: (0, 0))
    parts = [(g * (n_prompts // n), n_prompts // n) for n in (n_halves, n_quarters) for g in range(n)]
    return pl.pallas_call(
        functools.partial(norm_kernel, n_halves, n_prompts),
        grid=(n_prompts,),
        in_specs=[pl.BlockSpec((1, rows, width), lambda i: (i, 0, 0)), vec, vec, vec, vec],
        out_specs=[part_spec((rows, width), *part) for part in parts],
        out_shape=[jax.ShapeDtypeStruct((count, rows, width), jnp.bfloat16) for _, count in parts],
        compiler_params=pltpu.CompilerParams(dimension_semantics=("arbitrary",)),
        cost_estimate=pl.CostEstimate(flops=n_prompts * rows * width * 200, bytes_accessed=n_prompts * rows * width * 6, transcendentals=0),
        name="norms",
    )(hidden, g1, b1, g2, b2)


def turn_kernel(shard_ref, w_ref, out_ref):
    out_ref[...] = w_ref[...].T


def turned_columns(w, shard, n_shards):
    depth, columns = w.shape
    span, piece = columns // n_shards, 256
    return pl.pallas_call(
        turn_kernel,
        grid_spec=pltpu.PrefetchScalarGridSpec(
            num_scalar_prefetch=1,
            grid=(depth // piece,),
            in_specs=[pl.BlockSpec((piece, span), lambda i, shard: (i, shard[0]))],
            out_specs=pl.BlockSpec((span, piece), lambda i, shard: (0, i)),
        ),
        out_shape=jax.ShapeDtypeStruct((span, depth), w.dtype),
        cost_estimate=pl.CostEstimate(flops=depth * span * 1000, bytes_accessed=depth * span * 4, transcendentals=0),
        name="turn",
    )(shard, w)


def attn_kernel(n_heads, head_dim, rows, prev, info_ref, len_ref, a0, a1, a2, a3, w_ref, bias_ref, keep_ref, below_ref, above_ref, *rest):
    k_out, v_out, c0, c1, c2, c3, qkv_a, qkv_b, k_turned, ctx_buf = rest[prev:]
    step = pl.program_id(0)
    me = info_ref[0]
    sources = (a0, a1, a2, a3)
    n_blocks = len(sources)
    scale = LOG2_E * head_dim ** -0.5
    half_rot = head_dim // 8
    turning = keep_ref.shape[0]
    span = 3 * head_dim

    length = len_ref[step + info_ref[1]]
    key = lax.broadcasted_iota(jnp.int32, (rows, rows), 0)
    causal = key <= lax.broadcasted_iota(jnp.int32, (rows, rows), 1)

    def project(head, j, qkv):
        at = pl.ds(pl.multiple_of((me ^ j) * rows, rows), rows)
        w_rows = w_ref[pl.ds(pl.multiple_of(head * span, span), span)]
        out = lax.dot_general(w_rows, sources[j][0], (((1,), (1,)), ((), ())), preferred_element_type=jnp.float32) + bias_ref[head]
        keep, below, above = keep_ref[:, at], below_ref[:, at], above_ref[:, at]

        def rotate(u):
            first = u[:turning]
            first = first * keep + pltpu.roll(first, turning - half_rot, 0) * below + pltpu.roll(first, half_rot, 0) * above
            return jnp.concatenate([first, u[turning:]], axis=0).astype(jnp.bfloat16)

        k_cols = rotate(out[head_dim:2 * head_dim])
        v_cols = out[2 * head_dim:].astype(jnp.bfloat16)
        qkv[:head_dim, at] = rotate(out[:head_dim])
        qkv[head_dim:2 * head_dim, at] = k_cols
        qkv[2 * head_dim:, at] = v_cols
        k_out[0, head, :, at] = k_cols
        v_out[0, head, :, at] = v_cols

    def turn(qkv):
        k_turned[...] = qkv[head_dim:2 * head_dim].T

    def score(block, qkv):
        q_cols = qkv[:head_dim, pl.ds(block * rows, rows)]
        parts = []
        for j in range(block + 1):
            s = jnp.dot(k_turned[pl.ds(j * rows, rows)], q_cols, preferred_element_type=jnp.float32)
            if j == block:
                s = jnp.where(causal, s, -jnp.inf)
            if (j + 1) * rows > n_blocks * rows // 2:
                s = jnp.where(key < length - j * rows, s, -jnp.inf)
            parts.append(s)
        return parts

    def mix(head, block, qkv, parts):
        at = pl.ds(block * rows, rows)
        top = functools.reduce(jnp.maximum, parts)
        top = jnp.max(top, axis=0, keepdims=True)
        parts = [jnp.exp2((s - top) * scale) for s in parts]
        total = jnp.sum(functools.reduce(jnp.add, parts), axis=0, keepdims=True)
        weights = jnp.concatenate([p.astype(jnp.bfloat16) for p in parts], axis=0)
        context = jnp.dot(qkv[2 * head_dim:, pl.ds(0, (block + 1) * rows)], weights, preferred_element_type=jnp.float32)
        ctx_buf[pl.ds(pl.multiple_of(head * head_dim, head_dim), head_dim), at] = (context / total).astype(jnp.bfloat16)

    def head_step(head, qkv, next_head, next_qkv):
        turn(qkv)
        parts = score(0, qkv)
        for block in range(n_blocks):
            after = score(block + 1, qkv) if block + 1 < n_blocks else None
            project(next_head, block, next_qkv)
            mix(head, block, qkv, parts)
            parts = after

    for j in range(n_blocks):
        project(0, j, qkv_a)

    def pair(t, carry):
        head_step(2 * t, qkv_a, 2 * t + 1, qkv_b)
        head_step(2 * t + 1, qkv_b, 2 * t + 2, qkv_a)
        return carry

    lax.fori_loop(0, n_heads // 2 - 1, pair, 0)
    head_step(n_heads - 2, qkv_a, n_heads - 1, qkv_b)
    turn(qkv_b)
    parts = score(0, qkv_b)
    for block in range(n_blocks):
        after = score(block + 1, qkv_b) if block + 1 < n_blocks else None
        mix(n_heads - 1, block, qkv_b, parts)
        parts = after

    for j, out in enumerate((c0, c1, c2, c3)):
        out[0] = ctx_buf[:, pl.ds(pl.multiple_of((me ^ j) * rows, rows), rows)].T


def whole(shape):
    return pl.BlockSpec(shape, lambda i, *_: (0,) * len(shape), pipeline_mode=pl.Buffered(1))


def attention(info, lens, sources, w_turned, bias, tables, caches, n_prompts, first):
    count, rows, width = sources[0].shape
    n_heads, span, _ = bias.shape
    head_dim = span // 3
    seq = rows * len(sources)
    prev = 0 if caches is None else 2
    hbm = pl.BlockSpec(memory_space=pl.ANY)
    source_spec = pl.BlockSpec((1, rows, width), lambda i, *_: (i, 0, 0))
    table = whole(tables[0].shape)
    cache_shape = jax.ShapeDtypeStruct((n_prompts, n_heads, head_dim, seq), jnp.bfloat16)
    cache_spec = pl.BlockSpec((1, n_heads, head_dim, seq), lambda i, *_: (i + first, 0, 0, 0))
    ctx_shape = jax.ShapeDtypeStruct((count, rows, n_heads * head_dim), jnp.bfloat16)
    ctx_spec = pl.BlockSpec((1, rows, n_heads * head_dim), lambda i, *_: (i, 0, 0))
    columns = pltpu.VMEM((span, seq), jnp.bfloat16)
    flops = count * seq * width * n_heads * 256 * 2 + count * n_heads * seq * seq * 256 * 2
    return pl.pallas_call(
        functools.partial(attn_kernel, n_heads, head_dim, rows, prev),
        grid_spec=pltpu.PrefetchScalarGridSpec(
            num_scalar_prefetch=2,
            grid=(count,),
            in_specs=[source_spec] * 4 + [whole(w_turned.shape), whole(bias.shape), table, table, table] + [hbm] * prev,
            out_specs=[cache_spec, cache_spec] + [ctx_spec] * 4,
            scratch_shapes=[columns, columns, pltpu.VMEM((seq, head_dim), jnp.bfloat16), pltpu.VMEM((n_heads * head_dim, seq), jnp.bfloat16)],
        ),
        out_shape=[cache_shape, cache_shape] + [ctx_shape] * 4,
        input_output_aliases={11: 0, 12: 1} if prev else {},
        compiler_params=pltpu.CompilerParams(dimension_semantics=("arbitrary",), vmem_limit_bytes=58 * 1024 * 1024),
        cost_estimate=pl.CostEstimate(flops=flops, bytes_accessed=count * seq * width * 4, transcendentals=count * n_heads * seq * seq // 2),
        name="qkv_attention",
    )(info, lens, *sources, w_turned, bias, *tables, *(caches or ()))


def out_kernel(n_shards, n_halves, n_quarters, n_prompts, shard_ref, x_ref, b_out_ref, b_down_ref, *rest):
    mlps, rest = rest[:n_quarters], rest[n_quarters:]
    contexts, weights, out_ref = rest[:n_halves * n_shards], rest[n_halves * n_shards:-1], rest[-1]
    step = pl.program_id(0)
    for q in range(n_quarters):
        half = q * n_halves // n_quarters

        @pl.when(step // (n_prompts // n_quarters) == q)
        def _(q=q, half=half):
            attn = b_out_ref[...]
            for c_ref, w_ref in zip(contexts[half * n_shards:(half + 1) * n_shards], weights):
                attn = attn + jnp.dot(c_ref[0], w_ref[...], preferred_element_type=jnp.float32)
            out_ref[0] = (x_ref[0].astype(jnp.float32) + attn + (mlps[q][0] + b_down_ref[...])).astype(jnp.bfloat16)


def finish(shard, hidden, mlps, b_out, b_down, contexts, w_out):
    n_shards, n_halves, n_quarters = len(contexts[0]), len(contexts), len(mlps)
    n_prompts, rows, width = hidden.shape
    span = contexts[0][0].shape[-1]
    block = pl.BlockSpec((1, rows, width), lambda i, *_: (i, 0, 0))
    w_specs = [
        pl.BlockSpec((span, width), lambda i, shard, j=j: (shard[0] ^ j, 0), pipeline_mode=pl.Buffered(1)) for j in range(n_shards)
    ]
    half, quarter = n_prompts // n_halves, n_prompts // n_quarters
    ctx_specs = [part_spec((rows, span), g * half, half) for g in range(n_halves) for _ in range(n_shards)]
    mlp_specs = [part_spec((rows, width), g * quarter, quarter) for g in range(n_quarters)]
    return pl.pallas_call(
        functools.partial(out_kernel, n_shards, n_halves, n_quarters, n_prompts),
        grid_spec=pltpu.PrefetchScalarGridSpec(
            num_scalar_prefetch=1,
            grid=(n_prompts,),
            in_specs=[block, whole((1, width)), whole((1, width))] + mlp_specs + ctx_specs + w_specs,
            out_specs=block,
        ),
        out_shape=jax.ShapeDtypeStruct(hidden.shape, jnp.bfloat16),
        compiler_params=pltpu.CompilerParams(dimension_semantics=("arbitrary",), vmem_limit_bytes=60 * 1024 * 1024),
        cost_estimate=pl.CostEstimate(flops=n_prompts * rows * width * width * 2, bytes_accessed=n_prompts * rows * width * 10, transcendentals=0),
        name="finish",
    )(shard, hidden, b_out, b_down, *mlps, *(c for group in contexts for c in group), *([w_out] * n_shards))


def solution(mesh):
    n_shards = mesh.shape['sp']
    row_spec = P('dp', 'sp', None)
    cache_spec = P('dp', 'sp', None, None)
    vec_spec = P(None)
    mat_spec = P(None, None)

    def swap(array, mask):
        return lax.ppermute(array, 'sp', [(i, i ^ mask) for i in range(n_shards)])

    def layer(hidden, seq_lens, ln1_gain, ln1_bias, ln2_gain, ln2_bias, w_qkv, b_qkv, w_out, b_out, w_up, b_up, w_down, b_down):
        n_prompts, rows, width = hidden.shape
        n_heads, _, head_dim = b_qkv.shape
        own_heads = n_heads // n_shards
        shard = lax.axis_index('sp')
        n_halves, n_quarters = 2, 4
        half = n_prompts // n_halves

        normed = norms(hidden, n_halves, n_quarters, ln1_gain[None], ln1_bias[None], ln2_gain[None], ln2_bias[None])
        attn_ins, mlp_ins = normed[:n_halves], list(normed[n_halves:])
        gathered = []
        for attn_in in attn_ins:
            near = swap(attn_in, 1)
            far = swap(attn_in, 2)
            relay = swap(far, 1)
            gathered.append((attn_in, near, far, relay))

        where = shard.astype(jnp.int32).reshape(1)
        w_turned = turned_columns(w_qkv, where, n_shards)
        b_heads = lax.dynamic_slice_in_dim(b_qkv, shard * own_heads, own_heads, axis=0).reshape(own_heads, 3 * head_dim, 1)
        tables = rotary_tables(rows * n_shards, head_dim)

        def mlp(m):
            count = m.shape[0]
            pre = jnp.dot(m.reshape(count * rows, width), w_up, preferred_element_type=jnp.float32) + b_up
            act = (0.5 * pre * (1.0 + lax.erf(pre * (0.5 ** 0.5)))).astype(jnp.bfloat16)
            return jnp.dot(act, w_down, preferred_element_type=jnp.float32).reshape(count, rows, width)

        mlps = [mlp(mlp_ins[q]) for q in range(n_quarters - 1)]
        caches, contexts = None, []
        for g, sources in enumerate(gathered):
            info = jnp.stack([shard, jnp.int32(g * half)]).astype(jnp.int32)
            k_cache, v_cache, *ctx = attention(info, seq_lens, sources, w_turned, b_heads, tables, caches, n_prompts, g * half)
            caches = (k_cache, v_cache)
            if g == 1:
                mlp_ins[-1], *ctx = lax.optimization_barrier((mlp_ins[-1], *ctx))
            swapped = [ctx[0]]
            for j in range(1, n_shards):
                swapped.append(swap(ctx[j], j))
            contexts.append(swapped)
        mlps.append(mlp(mlp_ins[-1]))
        out = finish(where, hidden, mlps, b_out[None], b_down[None], contexts, w_out)
        return out, jnp.swapaxes(caches[0], 2, 3), jnp.swapaxes(caches[1], 2, 3)

    return jax.shard_map(layer, mesh=mesh,
                         in_specs=(row_spec, P('dp'), vec_spec, vec_spec, vec_spec, vec_spec, mat_spec, P(None, None, None), mat_spec, vec_spec, mat_spec, vec_spec, mat_spec, vec_spec),
                         out_specs=(row_spec, cache_spec, cache_spec), check_vma=False)
```

profile of v0, /device:TPU:0, one launch (start us, length us, event | category | flops | bytes accessed | tf_op | source)
XLA Modules:
  0.0 1140.3 jit_solution(15773085992131349691)
XLA Ops:
  0.6 1.3 broadcast_in_dim.32.g1_ref
  2.0 1.3 broadcast_in_dim.33.b1_ref
  3.3 1.3 broadcast_in_dim.34.g2_ref
  4.6 1.3 broadcast_in_dim.35.b2_ref
  5.9 35.1 %norms.1 = (bf16[8,256,2560]{2,1,0:T(8,128)(2,1)}, bf16[8,256,2560]{2,1,0:T(8,128)(2,1)}, bf16[4,256,2560]{2,1,0:T(8,128)(2,1)}, bf16[4,256,2560]{2,1,0:T(8,128)...) custom-call(bf16[16,256,2560]{2,1,0:T(8,128)(2,1)} %x_ref.3, f32[1,2560]{1,0:T(1,128)} %broadcast_in_dim.32.g1_ref, ...), custom_call_target="tpu_custom_call" | custom-call | flops 2097152000 | bytes 62914560 | tf_op jit(solution)/shard_map/norms/pallas_call | solution.py:54
  41.0 3.3 collective-permute-start.4
  46.0 1.4 reshape.56.bias_ref
  47.3 0.6 pad.10.clone
  47.9 0.6 pad.7.clone
  48.6 12.1 %turn.1.w_ref = bf16[1920,2560]{1,0:T(8,128)(2,1)} custom-call(s32[1]{0:T(128)} %bitcast.shard_ref, bf16[2560,7680]{1,0:T(8,128)(2,1)} %w_ref.1), custom_call_target="tpu_custom_call" | custom-call | flops 4915200000 | bytes 19660800 | tf_op jit(solution)/shard_map/turn/pallas_call | solution.py:73
  60.6 0.6 pad_add_fusion.1.info_ref
  61.3 0.6 pad_add_fusion.info_ref
  61.9 63.5 %multiply_convert_fusion.3.clone.2 = bf16[1024,10240]{1,0:T(8,128)(2,1)} fusion(bf16[1024,2560]{1,0:T(8,128)(2,1)} %bitcast.45, bf16[2560,10240]{1,0:T(8,128)(2,1)} %param.24, f32[10240]{0:T(1024)S(1)} %copy-done.17), kind=kOutput, calls=%fused_computation.3.clone.clone.clone | convolution fusion | flops 53750005760 | bytes 78684160 | tf_op jit(solution)/shard_map/dot_general | solution.py:287
  125.4 62.5 %multiply_convert_fusion.2.clone.2 = bf16[1024,10240]{1,0:T(8,128)(2,1)} fusion(bf16[1024,2560]{1,0:T(8,128)(2,1)S(1)} %bitcast.44, bf16[2560,10240]{1,0:T(8,128)(2,1)} %param.24, f32[10240]{0:T(1024)S(1)} %copy-done.17), kind=kOutput, calls=%fused_computation.2.clone.clone.clone | convolution fusion | flops 53750005760 | bytes 78684160 | tf_op jit(solution)/shard_map/dot_general | solution.py:287
  187.9 62.0 %multiply_convert_fusion.1.clone.2 = bf16[1024,10240]{1,0:T(8,128)(2,1)} fusion(bf16[1024,2560]{1,0:T(8,128)(2,1)S(1)} %bitcast.41, bf16[2560,10240]{1,0:T(8,128)(2,1)} %param.24, f32[10240]{0:T(1024)S(1)} %copy-done.17), kind=kOutput, calls=%fused_computation.1.clone.clone.clone | convolution fusion | flops 53750005760 | bytes 78684160 | tf_op jit(solution)/shard_map/dot_general | solution.py:287
  250.0 0.6 broadcast_in_dim.30.b_out_ref
  250.6 0.6 broadcast_in_dim.31.b_down_ref
  251.5 62.9 %fusion.3 = f32[1024,2560]{1,0:T(8,128)} fusion(bf16[10240,2560]{1,0:T(8,128)(2,1)} %param.26, bf16[1024,10240]{1,0:T(8,128)(2,1)} %multiply_convert_fusion.3.clone.2), kind=kOutput, calls=%fused_computation.7 | convolution fusion | flops 53687091200 | bytes 83886080 | tf_op jit(solution)/shard_map/dot_general | solution.py:289
  314.5 0.8 maximum_maximum_fusion.2
  315.2 62.6 %fusion.2 = f32[1024,2560]{1,0:T(8,128)} fusion(bf16[10240,2560]{1,0:T(8,128)(2,1)} %param.26, bf16[1024,10240]{1,0:T(8,128)(2,1)} %multiply_convert_fusion.2.clone.2), kind=kOutput, calls=%fused_computation.6 | convolution fusion | flops 53687091200 | bytes 83886080 | tf_op jit(solution)/shard_map/dot_general | solution.py:289
  377.9 62.8 %fusion.1 = f32[1024,2560]{1,0:T(8,128)} fusion(bf16[10240,2560]{1,0:T(8,128)(2,1)} %param.26, bf16[1024,10240]{1,0:T(8,128)(2,1)} %multiply_convert_fusion.1.clone.2), kind=kOutput, calls=%fused_computation.5 | convolution fusion | flops 53687091200 | bytes 83886080 | tf_op jit(solution)/shard_map/dot_general | solution.py:289
  440.7 54.0 %collective-permute-done.1.a2 = bf16[8,256,2560]{2,1,0:T(8,128)(2,1)} collective-permute-done((bf16[8,256,2560]{2,1,0:T(8,128)(2,1)}, bf16[8,256,2560]{2,1,0:T(8,128)(2,1)}, u32[]{:S(2)}, u32[]{:S(2)}) %collective-permute-start.1) | collective-permute-done | bytes 10485792 | tf_op jit(solution)/shard_map/ppermute | solution.py:261
  494.7 162.7 %qkv_attention.2 = (bf16[16,8,80,1024]{3,2,1,0:T(8,128)(2,1)}, bf16[16,8,80,1024]{3,2,1,0:T(8,128)(2,1)}, bf16[8,256,640]{2,1,0:T(8,128)(2,1)}, bf16[8,256,640]{...) custom-call(s32[2]{0:T(128)} %pad_add_fusion.1.info_ref, s32[16]{0:T(128)} %len_ref.3, ...), custom_call_target="tpu_custom_call" | custom-call | flops 120259084288 | bytes 83886080 | tf_op jit(solution)/shard_map/qkv_attention/pallas_call | solution.py:195
  657.5 163.5 %qkv_attention.3 = (bf16[16,8,80,1024]{3,2,1,0:T(8,128)(2,1)}, bf16[16,8,80,1024]{3,2,1,0:T(8,128)(2,1)}, bf16[8,256,640]{2,1,0:T(8,128)(2,1)}, bf16[8,256,640]{...) custom-call(s32[2]{0:T(128)} %pad_add_fusion.info_ref, ...), custom_call_target="tpu_custom_call", output_to_operand_aliasing={{0}: (11, {}), {1}: (12, {})} | custom-call | flops 120259084288 | bytes 83886080 | tf_op jit(solution)/shard_map/qkv_attention/pallas_call | solution.py:195
  821.0 1.8 collective-permute-start.10
  822.8 62.2 %multiply_convert_fusion.clone.4 = bf16[1024,10240]{1,0:T(8,128)(2,1)} fusion(bf16[1024,2560]{1,0:T(8,128)(2,1)S(1)} %bitcast.40, bf16[2560,10240]{1,0:T(8,128)(2,1)} %param.24, f32[10240]{0:T(1024)S(1)} %copy-done.18), kind=kOutput, calls=%fused_computation.clone.clone.clone.1 | convolution fusion | flops 53750005760 | bytes 78684160 | tf_op jit(solution)/shard_map/dot_general | solution.py:287
  885.8 1.4 collective-permute-start.7
  887.3 1.5 copy-done.13
  888.8 62.6 %fusion = f32[1024,2560]{1,0:T(8,128)} fusion(bf16[10240,2560]{1,0:T(8,128)(2,1)} %param.26, bf16[1024,10240]{1,0:T(8,128)(2,1)} %multiply_convert_fusion.clone.4), kind=kOutput, calls=%fused_computation.4 | convolution fusion | flops 53687091200 | bytes 83886080 | tf_op jit(solution)/shard_map/dot_general | solution.py:289
  951.4 49.3 %collective-permute-done.7.rest_6_ = bf16[8,256,640]{2,1,0:T(8,128)(2,1)} collective-permute-done((bf16[8,256,640]{2,1,0:T(8,128)(2,1)S(1)}, bf16[8,256,640]{2,1,0:T(8,128)(2,1)}, u32[]{:S(2)}, u32[]{:S(2)}) %collective-permute-start.7) | collective-permute-done | bytes 2621472 | tf_op jit(solution)/shard_map/ppermute | solution.py:261
  1000.7 55.5 %collective-permute-done.8.rest_7_ = bf16[8,256,640]{2,1,0:T(8,128)(2,1)} collective-permute-done((bf16[8,256,640]{2,1,0:T(8,128)(2,1)S(1)}, bf16[8,256,640]{2,1,0:T(8,128)(2,1)}, u32[]{:S(2)}, u32[]{:S(2)}) %collective-permute-start.8) | collective-permute-done | bytes 2621472 | tf_op jit(solution)/shard_map/ppermute | solution.py:261
  1056.2 83.8 %finish.1 = bf16[16,256,2560]{2,1,0:T(8,128)(2,1)} custom-call(s32[1]{0:T(128)} %bitcast.shard_ref, bf16[16,256,2560]{2,1,0:T(8,128)(2,1)} %x_ref.3, f32[1,2560]{1,0:T(1,128)} %broadcast_in_dim.30.b_out_ref, f32[1,2560]{1,0:T(1,128)} %broadcast_in_dim.31.b_down_ref, f32[4,256,2560]{2,1,0:T(8,128)} %bitcast.48, f32[4,256,2560]{2,1,0:T(8,128)} %bitcast.49, ...), custom_call_target="tpu_custom_call" | custom-call | flops 53687091200 | bytes 104857600 | tf_op jit(solution)/shard_map/finish/pallas_call | solution.py:238
  (68 shorter events, 3.0 us)
Async XLA Ops:
  0.6 45.3 %copy-start = (f32[32,3,80]{2,0,1:T(8,128)S(1)}, f32[32,3,80]{2,0,1:T(8,128)}, u32[]{:S(2)}) copy-start(f32[32,3,80]{2,0,1:T(8,128)} %param.21) | copy-start | bytes 92164
  41.0 336.8 %collective-permute-start.4 = (bf16[8,256,2560]{2,1,0:T(8,128)(2,1)}, bf16[8,256,2560]{2,1,0:T(8,128)(2,1)}, u32[]{:S(2)}, u32[]{:S(2)}) collective-permute-start(bf16[8,256,2560]{2,1,0:T(8,128)(2,1)} %get-tuple-element.31.a0), channel_id=1, source_target_pairs={{0,2},{1,3},{2,0},{3,1},{4,6},{5,7},{6,4},{7,5}} | collective-permute-start | bytes 31457288 | tf_op jit(solution)/shard_map/ppermute | solution.py:261
  44.3 450.4 %collective-permute-start.3 = (bf16[8,256,2560]{2,1,0:T(8,128)(2,1)}, bf16[8,256,2560]{2,1,0:T(8,128)(2,1)}, u32[]{:S(2)}, u32[]{:S(2)}) collective-permute-start(bf16[8,256,2560]{2,1,0:T(8,128)(2,1)} %get-tuple-element.31.a0), channel_id=1, source_target_pairs={{0,1},{1,0},{2,3},{3,2},{4,5},{5,4},{6,7},{7,6}} | collective-permute-start | bytes 31457288 | tf_op jit(solution)/shard_map/ppermute | solution.py:261
  44.3 450.4 %collective-permute-start.1 = (bf16[8,256,2560]{2,1,0:T(8,128)(2,1)}, bf16[8,256,2560]{2,1,0:T(8,128)(2,1)}, u32[]{:S(2)}, u32[]{:S(2)}) collective-permute-start(bf16[8,256,2560]{2,1,0:T(8,128)(2,1)} %get-tuple-element.30.a0), channel_id=1, source_target_pairs={{0,2},{1,3},{2,0},{3,1},{4,6},{5,7},{6,4},{7,5}} | collective-permute-start | bytes 31457288 | tf_op jit(solution)/shard_map/ppermute | solution.py:261
  44.4 613.0 %collective-permute-start = (bf16[8,256,2560]{2,1,0:T(8,128)(2,1)}, bf16[8,256,2560]{2,1,0:T(8,128)(2,1)}, u32[]{:S(2)}, u32[]{:S(2)}) collective-permute-start(bf16[8,256,2560]{2,1,0:T(8,128)(2,1)} %get-tuple-element.30.a0), channel_id=1, source_target_pairs={{0,1},{1,0},{2,3},{3,2},{4,5},{5,4},{6,7},{7,6}} | collective-permute-start | bytes 31457288 | tf_op jit(solution)/shard_map/ppermute | solution.py:261
  48.6 13.3 %copy-start.17 = (f32[10240]{0:T(1024)S(1)}, f32[10240]{0:T(1024)}, u32[]{:S(2)}) copy-start(f32[10240]{0:T(1024)} %param.25) | copy-start | bytes 122884
  48.6 76.8 %slice-start = ((s8[5242880]{0:T(1024)(128)(4,1)}), s8[1048576]{0:T(1024)(128)(4,1)S(1)}, s32[]{:S(2)}) async-start(s8[5242880]{0:T(1024)(128)(4,1)} %bitcast.42), calls=%async_computation | async-start | bytes 2097152
  61.9 63.5 %slice-start.1 = ((s8[5242880]{0:T(1024)(128)(4,1)}), s8[4194304]{0:T(1024)(128)(4,1)S(1)}, s32[]{:S(2)}) async-start(s8[5242880]{0:T(1024)(128)(4,1)} %bitcast.42), calls=%async_computation.1 | async-start | bytes 8388608
  125.4 62.5 %copy-start.9 = (bf16[4,256,2560]{2,1,0:T(8,128)(2,1)S(1)}, bf16[4,256,2560]{2,1,0:T(8,128)(2,1)}, u32[]{:S(2)}) copy-start(bf16[4,256,2560]{2,1,0:T(8,128)(2,1)} %get-tuple-element.28) | copy-start | bytes 15728644
  187.9 62.1 %copy-start.3 = (f32[2560]{0:T(1024)S(1)}, f32[2560]{0:T(1024)}, u32[]{:S(2)}) copy-start(f32[2560]{0:T(1024)} %param.23) | copy-start | bytes 30724
  187.9 62.7 %copy-start.4 = (f32[2560]{0:T(1024)S(1)}, f32[2560]{0:T(1024)}, u32[]{:S(2)}) copy-start(f32[2560]{0:T(1024)} %param.27) | copy-start | bytes 30724
  187.9 63.3 %copy-start.2 = (f32[1024]{0:T(1024)S(1)}, f32[1024]{0:T(1024)}, u32[]{:S(2)}) copy-start(f32[1024]{0:T(1024)} %iota_convert_fusion) | copy-start | bytes 12292
  187.9 63.3 %copy-start.5 = (f32[10]{0:T(128)S(1)}, f32[10]{0:T(128)}, u32[]{:S(2)}) copy-start(f32[10]{0:T(128)} %multiply_power_fusion) | copy-start | bytes 124
  251.5 62.9 %copy-start.6 = (f32[24]{0:T(128)S(1)}, f32[24]{0:T(128)}, u32[]{:S(2)}) copy-start(f32[24]{0:T(128)} %pad.10.clone) | copy-start | bytes 292
  251.5 62.9 %copy-start.7 = (f32[24]{0:T(128)S(1)}, f32[24]{0:T(128)}, u32[]{:S(2)}) copy-start(f32[24]{0:T(128)} %pad.7.clone) | copy-start | bytes 292
  377.8 116.9 %collective-permute-start.5 = (bf16[8,256,2560]{2,1,0:T(8,128)(2,1)}, bf16[8,256,2560]{2,1,0:T(8,128)(2,1)}, u32[]{:S(2)}, u32[]{:S(2)}) collective-permute-start(bf16[8,256,2560]{2,1,0:T(8,128)(2,1)} %collective-permute-done.4.a2), channel_id=1, source_target_pairs={{0,1},{1,0},{2,3},{3,2},{4,5},{5,4},{6,7},{7,6}} | collective-permute-start | bytes 31457288 | tf_op jit(solution)/shard_map/ppermute | solution.py:261
  494.7 162.7 %collective-permute-start.2 = (bf16[8,256,2560]{2,1,0:T(8,128)(2,1)}, bf16[8,256,2560]{2,1,0:T(8,128)(2,1)}, u32[]{:S(2)}, u32[]{:S(2)}) collective-permute-start(bf16[8,256,2560]{2,1,0:T(8,128)(2,1)} %collective-permute-done.1.a2), channel_id=1, source_target_pairs={{0,1},{1,0},{2,3},{3,2},{4,5},{5,4},{6,7},{7,6}} | collective-permute-start | bytes 31457288 | tf_op jit(solution)/shard_map/ppermute | solution.py:261
  657.4 165.3 %copy-start.8 = (bf16[4,256,2560]{2,1,0:T(8,128)(2,1)S(1)}, bf16[4,256,2560]{2,1,0:T(8,128)(2,1)}, u32[]{:S(2)}) copy-start(bf16[4,256,2560]{2,1,0:T(8,128)(2,1)} %get-tuple-element.38) | copy-start | bytes 15728644
  657.4 165.3 %copy-start.18 = (f32[10240]{0:T(1024)S(1)}, f32[10240]{0:T(1024)}, u32[]{:S(2)}) copy-start(f32[10240]{0:T(1024)} %param.25) | copy-start | bytes 122884
  821.0 66.3 %collective-permute-start.10 = (bf16[8,256,640]{2,1,0:T(8,128)(2,1)}, bf16[8,256,640]{2,1,0:T(8,128)(2,1)S(1)}, u32[]{:S(2)}, u32[]{:S(2)}) collective-permute-start(bf16[8,256,640]{2,1,0:T(8,128)(2,1)} %get-tuple-element.45), channel_id=1, source_target_pairs={{0,2},{1,3},{2,0},{3,1},{4,6},{5,7},{6,4},{7,5}} | collective-permute-start | bytes 7864328 | tf_op jit(solution)/shard_map/ppermute | solution.py:261
  822.7 62.2 %copy-start.16 = (bf16[8,256,640]{2,1,0:T(8,128)(2,1)S(1)}, bf16[8,256,640]{2,1,0:T(8,128)(2,1)}, u32[]{:S(2)}) copy-start(bf16[8,256,640]{2,1,0:T(8,128)(2,1)} %get-tuple-element.46) | copy-start | bytes 7864324
  822.7 62.5 %copy-start.14 = (bf16[8,256,640]{2,1,0:T(8,128)(2,1)S(1)}, bf16[8,256,640]{2,1,0:T(8,128)(2,1)}, u32[]{:S(2)}) copy-start(bf16[8,256,640]{2,1,0:T(8,128)(2,1)} %get-tuple-element.44) | copy-start | bytes 7864324
  822.8 62.6 %copy-start.12 = (bf16[8,256,640]{2,1,0:T(8,128)(2,1)S(1)}, bf16[8,256,640]{2,1,0:T(8,128)(2,1)}, u32[]{:S(2)}) copy-start(bf16[8,256,640]{2,1,0:T(8,128)(2,1)} %get-tuple-element.40) | copy-start | bytes 7864324
  822.8 63.0 %copy-start.11 = (bf16[8,256,640]{2,1,0:T(8,128)(2,1)S(1)}, bf16[8,256,640]{2,1,0:T(8,128)(2,1)}, u32[]{:S(2)}) copy-start(bf16[8,256,640]{2,1,0:T(8,128)(2,1)} %get-tuple-element.41) | copy-start | bytes 7864324
  822.8 66.0 %copy-start.10 = (bf16[8,256,640]{2,1,0:T(8,128)(2,1)S(1)}, bf16[8,256,640]{2,1,0:T(8,128)(2,1)}, u32[]{:S(2)}) copy-start(bf16[8,256,640]{2,1,0:T(8,128)(2,1)} %get-tuple-element.42) | copy-start | bytes 7864324
  885.0 66.4 %collective-permute-start.11 = (bf16[8,256,640]{2,1,0:T(8,128)(2,1)S(1)}, bf16[8,256,640]{2,1,0:T(8,128)(2,1)S(1)}, u32[]{:S(2)}, u32[]{:S(2)}) collective-permute-start(bf16[8,256,640]{2,1,0:T(8,128)(2,1)S(1)} %copy-done.16), channel_id=1, source_target_pairs={{0,3},{1,2},{2,1},{3,0},{4,7},{5,6},{6,5},{7,4}} | collective-permute-start | bytes 7864328 | tf_op jit(solution)/shard_map/ppermute | solution.py:261
  885.3 66.1 %collective-permute-start.9 = (bf16[8,256,640]{2,1,0:T(8,128)(2,1)S(1)}, bf16[8,256,640]{2,1,0:T(8,128)(2,1)}, u32[]{:S(2)}, u32[]{:S(2)}) collective-permute-start(bf16[8,256,640]{2,1,0:T(8,128)(2,1)S(1)} %copy-done.14), channel_id=1, source_target_pairs={{0,1},{1,0},{2,3},{3,2},{4,5},{5,4},{6,7},{7,6}} | collective-permute-start | bytes 7864328 | tf_op jit(solution)/shard_map/ppermute | solution.py:261
  885.4 66.1 %collective-permute-start.6 = (bf16[8,256,640]{2,1,0:T(8,128)(2,1)S(1)}, bf16[8,256,640]{2,1,0:T(8,128)(2,1)}, u32[]{:S(2)}, u32[]{:S(2)}) collective-permute-start(bf16[8,256,640]{2,1,0:T(8,128)(2,1)S(1)} %copy-done.12), channel_id=1, source_target_pairs={{0,1},{1,0},{2,3},{3,2},{4,5},{5,4},{6,7},{7,6}} | collective-permute-start | bytes 7864328 | tf_op jit(solution)/shard_map/ppermute | solution.py:261
  885.8 114.9 %collective-permute-start.7 = (bf16[8,256,640]{2,1,0:T(8,128)(2,1)S(1)}, bf16[8,256,640]{2,1,0:T(8,128)(2,1)}, u32[]{:S(2)}, u32[]{:S(2)}) collective-permute-start(bf16[8,256,640]{2,1,0:T(8,128)(2,1)S(1)} %copy-done.11), channel_id=1, source_target_pairs={{0,2},{1,3},{2,0},{3,1},{4,6},{5,7},{6,4},{7,5}} | collective-permute-start | bytes 7864328 | tf_op jit(solution)/shard_map/ppermute | solution.py:261
  888.8 167.5 %collective-permute-start.8 = (bf16[8,256,640]{2,1,0:T(8,128)(2,1)S(1)}, bf16[8,256,640]{2,1,0:T(8,128)(2,1)}, u32[]{:S(2)}, u32[]{:S(2)}) collective-permute-start(bf16[8,256,640]{2,1,0:T(8,128)(2,1)S(1)} %copy-done.10), channel_id=1, source_target_pairs={{0,3},{1,2},{2,1},{3,0},{4,7},{5,6},{6,5},{7,4}} | collective-permute-start | bytes 7864328 | tf_op jit(solution)/shard_map/ppermute | solution.py:261
  951.4 104.8 %copy-start.15 = (bf16[8,256,640]{2,1,0:T(8,128)(2,1)}, bf16[8,256,640]{2,1,0:T(8,128)(2,1)S(1)}, u32[]{:S(2)}) copy-start(bf16[8,256,640]{2,1,0:T(8,128)(2,1)S(1)} %collective-permute-done.11.rest_11_) | copy-start | bytes 7864324
  1056.2 83.8 %copy-start.1 = (f32[32,3,80]{2,0,1:T(8,128)S(1)}, f32[32,3,80]{2,0,1:T(8,128)}, u32[]{:S(2)}) copy-start(f32[32,3,80]{2,0,1:T(8,128)} %param.21) | copy-start | bytes 92164
  (1 other events, 1.5 us)
where the time goes:
time: 1150 us; the launch traced here: 1140 us
  matrix products  501 us (44%)
  Pallas kernels  457 us (40%)
  waiting for transfers between devices  159 us (14%)
    pallas_call x2, Pallas kernels, attention(): pl.pallas_call(functools.partial(attn_kernel, n_heads, head_dim, rows, pr...  326 us
    dot_general x4, matrix products, mlp(): jnp.dot(act, w_down, preferred_element_type=jnp.float32)  251 us
    dot_general x4, matrix products, mlp(): jnp.dot(m.reshape(count * rows, width), w_up, preferred_element_type=jnp....  250 us
    ppermute x12, waiting for transfers between devices, swap(): return lax.ppermute(array, 'sp', [(i, i ^ mask) for i in range(n_shards)])  159 us
    pallas_call x1, Pallas kernels, finish(): pl.pallas_call(functools.partial(out_kernel, n_shards, n_halves, n_quarte...  83.8 us
    pallas_call x1, Pallas kernels, norms(): pl.pallas_call(functools.partial(norm_kernel, n_halves, n_prompts), grid=...  35.1 us
  transfers between devices with their start and end apart: 12, of which 3 were waited for; matrix products, arithmetic and copies ran while one was open for 45% of the time, Pallas kernels for 15%

commit v1 on v0

--- a/solution.py
+++ b/solution.py
@@ -27,20 +27,24 @@
     return keep, below, above
 
 
-def norm_kernel(n_halves, n_prompts, x_ref, g1_ref, b1_ref, g2_ref, b2_ref, *outs):
+def norm_kernel(n_halves, n_quarters, n_prompts, x_ref, g1_ref, b1_ref, g2_ref, b2_ref, *outs):
     step = pl.program_id(0)
-    rows = x_ref[0].astype(jnp.float32)
-    centered = rows - jnp.mean(rows, axis=-1, keepdims=True)
-    variance = jnp.mean(centered * centered, axis=-1, keepdims=True)
-    normed = centered * lax.rsqrt(variance + LN_EPS)
-    a_rows = (normed * g1_ref[...] + b1_ref[...]).astype(jnp.bfloat16)
-    m_rows = (normed * g2_ref[...] + b2_ref[...]).astype(jnp.bfloat16)
-    for parts, result in ((outs[:n_halves], a_rows), (outs[n_halves:], m_rows)):
-        size = n_prompts // len(parts)
-        for g, part in enumerate(parts):
-            @pl.when(step // size == g)
-            def _(part=part, result=result):
-                part[0] = result
+    n_rows, piece = x_ref.shape[1], 16
+
+    def run(a_part, m_part):
+        for start in range(0, n_rows, piece):
+            at = pl.ds(start, piece)
+            rows = x_ref[0, at].astype(jnp.float32)
+            centered = rows - jnp.mean(rows, axis=-1, keepdims=True)
+            variance = jnp.mean(centered * centered, axis=-1, keepdims=True)
+            normed = centered * lax.rsqrt(variance + LN_EPS)
+            a_part[0, at] = (normed * g1_ref[...] + b1_ref[...]).astype(jnp.bfloat16)
+            m_part[0, at] = (normed * g2_ref[...] + b2_ref[...]).astype(jnp.bfloat16)
+
+    for q in range(n_quarters):
+        @pl.when(step // (n_prompts // n_quarters) == q)
+        def _(q=q):
+            run(outs[q * n_halves // n_quarters], outs[n_halves + q])
 
 
 def part_spec(shape, start, count):
@@ -52,7 +56,7 @@
     vec = pl.BlockSpec((1, width), lambda i: (0, 0))
     parts = [(g * (n_prompts // n), n_prompts // n) for n in (n_halves, n_quarters) for g in range(n)]
     return pl.pallas_call(
-        functools.partial(norm_kernel, n_halves, n_prompts),
+        functools.partial(norm_kernel, n_halves, n_quarters, n_prompts),
         grid=(n_prompts,),
         in_specs=[pl.BlockSpec((1, rows, width), lambda i: (i, 0, 0)), vec, vec, vec, vec],
         out_specs=[part_spec((rows, width), *part) for part in parts],
@@ -211,16 +215,17 @@
 
 def out_kernel(n_shards, n_halves, n_quarters, n_prompts, shard_ref, x_ref, b_out_ref, b_down_ref, *rest):
     mlps, rest = rest[:n_quarters], rest[n_quarters:]
-    contexts, weights, out_ref = rest[:n_halves * n_shards], rest[n_halves * n_shards:-1], rest[-1]
-    step = pl.program_id(0)
+    contexts, (w_ref, out_ref, ctx_buf) = rest[:n_halves * n_shards], rest[n_halves * n_shards:]
+    step, me = pl.program_id(0), shard_ref[0]
     for q in range(n_quarters):
         half = q * n_halves // n_quarters
 
         @pl.when(step // (n_prompts // n_quarters) == q)
         def _(q=q, half=half):
-            attn = b_out_ref[...]
-            for c_ref, w_ref in zip(contexts[half * n_shards:(half + 1) * n_shards], weights):
-                attn = attn + jnp.dot(c_ref[0], w_ref[...], preferred_element_type=jnp.float32)
+            for j, c_ref in enumerate(contexts[half * n_shards:(half + 1) * n_shards]):
+                span = c_ref.shape[-1]
+                ctx_buf[:, pl.ds(pl.multiple_of((me ^ j) * span, span), span)] = c_ref[0]
+            attn = jnp.dot(ctx_buf[...], w_ref[...], preferred_element_type=jnp.float32) + b_out_ref[...]
             out_ref[0] = (x_ref[0].astype(jnp.float32) + attn + (mlps[q][0] + b_down_ref[...])).astype(jnp.bfloat16)
 
 
@@ -229,9 +234,6 @@
     n_prompts, rows, width = hidden.shape
     span = contexts[0][0].shape[-1]
     block = pl.BlockSpec((1, rows, width), lambda i, *_: (i, 0, 0))
-    w_specs = [
-        pl.BlockSpec((span, width), lambda i, shard, j=j: (shard[0] ^ j, 0), pipeline_mode=pl.Buffered(1)) for j in range(n_shards)
-    ]
     half, quarter = n_prompts // n_halves, n_prompts // n_quarters
     ctx_specs = [part_spec((rows, span), g * half, half) for g in range(n_halves) for _ in range(n_shards)]
     mlp_specs = [part_spec((rows, width), g * quarter, quarter) for g in range(n_quarters)]
@@ -240,14 +242,15 @@
         grid_spec=pltpu.PrefetchScalarGridSpec(
             num_scalar_prefetch=1,
             grid=(n_prompts,),
-            in_specs=[block, whole((1, width)), whole((1, width))] + mlp_specs + ctx_specs + w_specs,
+            in_specs=[block, whole((1, width)), whole((1, width))] + mlp_specs + ctx_specs + [whole(w_out.shape)],
             out_specs=block,
+            scratch_shapes=[pltpu.VMEM((rows, width), jnp.bfloat16)],
         ),
         out_shape=jax.ShapeDtypeStruct(hidden.shape, jnp.bfloat16),
         compiler_params=pltpu.CompilerParams(dimension_semantics=("arbitrary",), vmem_limit_bytes=60 * 1024 * 1024),
         cost_estimate=pl.CostEstimate(flops=n_prompts * rows * width * width * 2, bytes_accessed=n_prompts * rows * width * 10, transcendentals=0),
         name="finish",
-    )(shard, hidden, b_out, b_down, *mlps, *(c for group in contexts for c in group), *([w_out] * n_shards))
+    )(shard, hidden, b_out, b_down, *mlps, *(c for group in contexts for c in group), w_out)
 
 
 def solution(mesh):
@@ -282,16 +285,19 @@
         b_heads = lax.dynamic_slice_in_dim(b_qkv, shard * own_heads, own_heads, axis=0).reshape(own_heads, 3 * head_dim, 1)
         tables = rotary_tables(rows * n_shards, head_dim)
 
-        def mlp(m):
-            count = m.shape[0]
-            pre = jnp.dot(m.reshape(count * rows, width), w_up, preferred_element_type=jnp.float32) + b_up
-            act = (0.5 * pre * (1.0 + lax.erf(pre * (0.5 ** 0.5)))).astype(jnp.bfloat16)
-            return jnp.dot(act, w_down, preferred_element_type=jnp.float32).reshape(count, rows, width)
-
-        mlps = [mlp(mlp_ins[q]) for q in range(n_quarters - 1)]
+        def up(q):
+            pre = jnp.dot(mlp_ins[q].reshape(-1, width), w_up, preferred_element_type=jnp.float32) + b_up
+            return (0.5 * pre * (1.0 + lax.erf(pre * (0.5 ** 0.5)))).astype(jnp.bfloat16)
+
+        def down(act):
+            return jnp.dot(act, w_down, preferred_element_type=jnp.float32).reshape(-1, rows, width)
+
+        acts = [up(q) for q in range(n_quarters - 1)]
+        where_first, acts[-1] = lax.optimization_barrier((where, acts[-1]))
+        mlps = [down(act) for act in acts]
         caches, contexts = None, []
         for g, sources in enumerate(gathered):
-            info = jnp.stack([shard, jnp.int32(g * half)]).astype(jnp.int32)
+            info = jnp.concatenate([where_first if g == 0 else where, jnp.full(1, g * half, jnp.int32)])
             k_cache, v_cache, *ctx = attention(info, seq_lens, sources, w_turned, b_heads, tables, caches, n_prompts, g * half)
             caches = (k_cache, v_cache)
             if g == 1:
@@ -300,7 +306,7 @@
             for j in range(1, n_shards):
                 swapped.append(swap(ctx[j], j))
             contexts.append(swapped)
-        mlps.append(mlp(mlp_ins[-1]))
+        mlps.append(down(up(n_quarters - 1)))
         out = finish(where, hidden, mlps, b_out[None], b_down[None], contexts, w_out)
         return out, jnp.swapaxes(caches[0], 2, 3), jnp.swapaxes(caches[1], 2, 3)
 

time: 1150 us -> 1140 us (level)
  Pallas kernels: 457 us -> 445 us
where the time goes in v1:
time: 1140 us; the launch traced here: 1130 us
  matrix products  502 us (44%)
  Pallas kernels  445 us (39%)
  waiting for transfers between devices  157 us (14%)
    pallas_call x2, Pallas kernels, attention(): pl.pallas_call(functools.partial(attn_kernel, n_heads, head_dim, rows, pr...  326 us
    dot_general x4, matrix products, up(): jnp.dot(mlp_ins[q].reshape(-1, width), w_up, preferred_element_type=jnp.f...  251 us
    dot_general x4, matrix products, down(): jnp.dot(act, w_down, preferred_element_type=jnp.float32)  251 us
    ppermute x12, waiting for transfers between devices, swap(): return lax.ppermute(array, 'sp', [(i, i ^ mask) for i in range(n_shards)])  157 us
    pallas_call x1, Pallas kernels, finish(): pl.pallas_call(functools.partial(out_kernel, n_shards, n_halves, n_quarte...  73.5 us
    pallas_call x1, Pallas kernels, norms(): pl.pallas_call(functools.partial(norm_kernel, n_halves, n_quarters, n_pro...  33.8 us
  transfers between devices with their start and end apart: 12, of which 3 were waited for; matrix products, arithmetic and copies ran while one was open for 45% of the time, Pallas kernels for 15%

profile of v1, /device:TPU:0, one launch (start us, length us, event | category | flops | bytes accessed | tf_op | source)
XLA Modules:
  0.0 1128.5 jit_solution(10657468799264855991)
XLA Ops:
  0.7 1.3 broadcast_in_dim.32.g1_ref
  2.0 1.3 broadcast_in_dim.33.b1_ref
  3.3 1.3 broadcast_in_dim.34.g2_ref
  4.6 1.3 broadcast_in_dim.35.b2_ref
  5.9 33.8 %norms.1 = (bf16[8,256,2560]{2,1,0:T(8,128)(2,1)}, bf16[8,256,2560]{2,1,0:T(8,128)(2,1)}, bf16[4,256,2560]{2,1,0:T(8,128)(2,1)}, bf16[4,256,2560]{2,1,0:T(8,128)...) custom-call(bf16[16,256,2560]{2,1,0:T(8,128)(2,1)} %x_ref.3, f32[1,2560]{1,0:T(1,128)} %broadcast_in_dim.32.g1_ref, ...), custom_call_target="tpu_custom_call" | custom-call | flops 2097152000 | bytes 62914560 | tf_op jit(solution)/shard_map/norms/pallas_call | solution.py:58
  39.8 3.3 collective-permute-start.4
  43.6 0.6 iota_convert_fusion
  44.2 0.6 multiply_power_fusion
  44.8 63.3 %multiply_convert_fusion.1 = bf16[1024,10240]{1,0:T(8,128)(2,1)} fusion(bf16[1024,2560]{1,0:T(8,128)(2,1)} %bitcast.43, bf16[2560,10240]{1,0:T(8,128)(2,1)} %param.24, f32[10240]{0:T(1024)S(1)} %copy-done.16), kind=kOutput, calls=%fused_computation.1 | convolution fusion | flops 53750005760 | bytes 78684160 | tf_op jit(solution)/shard_map/dot_general | solution.py:289
  108.1 1.4 reshape.56.bias_ref
  109.5 0.6 pad.10.clone
  110.7 12.0 %turn.1.w_ref = bf16[1920,2560]{1,0:T(8,128)(2,1)} custom-call(s32[1]{0:T(128)} %bitcast.shard_ref, bf16[2560,7680]{1,0:T(8,128)(2,1)} %w_ref.1), custom_call_target="tpu_custom_call" | custom-call | flops 4915200000 | bytes 19660800 | tf_op jit(solution)/shard_map/turn/pallas_call | solution.py:77
  123.2 64.0 %multiply_convert_fusion.3.clone.2 = bf16[1024,10240]{1,0:T(8,128)(2,1)} fusion(bf16[1024,2560]{1,0:T(8,128)(2,1)} %bitcast.42, bf16[2560,10240]{1,0:T(8,128)(2,1)} %param.24, f32[10240]{0:T(1024)S(1)} %copy-done.16), kind=kOutput, calls=%fused_computation.3.clone.clone.clone | convolution fusion | flops 53750005760 | bytes 78684160 | tf_op jit(solution)/shard_map/dot_general | solution.py:289
  187.2 61.9 %multiply_convert_fusion.2.clone.2 = bf16[1024,10240]{1,0:T(8,128)(2,1)} fusion(bf16[1024,2560]{1,0:T(8,128)(2,1)S(1)} %bitcast.41, bf16[2560,10240]{1,0:T(8,128)(2,1)} %param.24, f32[10240]{0:T(1024)S(1)} %copy-done.16), kind=kOutput, calls=%fused_computation.2.clone.clone.clone | convolution fusion | flops 53750005760 | bytes 78684160 | tf_op jit(solution)/shard_map/dot_general | solution.py:289
  249.1 0.6 broadcast_in_dim.30.b_out_ref
  249.7 0.6 broadcast_in_dim.31.b_down_ref
  250.3 0.6 pad_add_fusion.1.info_ref
  251.3 62.9 %fusion.25 = f32[1024,2560]{1,0:T(8,128)} fusion(bf16[1024,10240]{1,0:T(8,128)(2,1)} %multiply_convert_fusion.1, bf16[10240,2560]{1,0:T(8,128)(2,1)} %param.26), kind=kOutput, calls=%fused_computation.39 | convolution fusion | flops 53687091200 | bytes 83886080 | tf_op jit(solution)/shard_map/dot_general | solution.py:293
  314.2 0.8 maximum_maximum_fusion.2
  315.1 62.7 %fusion.2 = f32[1024,2560]{1,0:T(8,128)} fusion(bf16[10240,2560]{1,0:T(8,128)(2,1)} %param.26, bf16[1024,10240]{1,0:T(8,128)(2,1)} %multiply_convert_fusion.3.clone.2), kind=kOutput, calls=%fused_computation.6 | convolution fusion | flops 53687091200 | bytes 83886080 | tf_op jit(solution)/shard_map/dot_general | solution.py:293
  377.8 62.8 %fusion.1 = f32[1024,2560]{1,0:T(8,128)} fusion(bf16[10240,2560]{1,0:T(8,128)(2,1)} %param.26, bf16[1024,10240]{1,0:T(8,128)(2,1)} %multiply_convert_fusion.2.clone.2), kind=kOutput, calls=%fused_computation.5 | convolution fusion | flops 53687091200 | bytes 83886080 | tf_op jit(solution)/shard_map/dot_general | solution.py:293
  440.7 52.8 %collective-permute-done.1.a2 = bf16[8,256,2560]{2,1,0:T(8,128)(2,1)} collective-permute-done((bf16[8,256,2560]{2,1,0:T(8,128)(2,1)}, bf16[8,256,2560]{2,1,0:T(8,128)(2,1)}, u32[]{:S(2)}, u32[]{:S(2)}) %collective-permute-start.1) | collective-permute-done | bytes 10485792 | tf_op jit(solution)/shard_map/ppermute | solution.py:264
  493.5 162.7 %qkv_attention.2 = (bf16[16,8,80,1024]{3,2,1,0:T(8,128)(2,1)}, bf16[16,8,80,1024]{3,2,1,0:T(8,128)(2,1)}, bf16[8,256,640]{2,1,0:T(8,128)(2,1)}, bf16[8,256,640]{...) custom-call(s32[2]{0:T(128)} %pad_add_fusion.1.info_ref, s32[16]{0:T(128)} %len_ref.3, ...), custom_call_target="tpu_custom_call" | custom-call | flops 120259084288 | bytes 83886080 | tf_op jit(solution)/shard_map/qkv_attention/pallas_call | solution.py:199
  656.2 163.5 %qkv_attention.3 = (bf16[16,8,80,1024]{3,2,1,0:T(8,128)(2,1)}, bf16[16,8,80,1024]{3,2,1,0:T(8,128)(2,1)}, bf16[8,256,640]{2,1,0:T(8,128)(2,1)}, bf16[8,256,640]{...) custom-call(s32[2]{0:T(128)} %pad_add_fusion.info_ref, ...), custom_call_target="tpu_custom_call", output_to_operand_aliasing={{0}: (11, {}), {1}: (12, {})} | custom-call | flops 120259084288 | bytes 83886080 | tf_op jit(solution)/shard_map/qkv_attention/pallas_call | solution.py:199
  819.7 1.7 collective-permute-start.10
  821.5 62.2 %multiply_convert_fusion.clone.4 = bf16[1024,10240]{1,0:T(8,128)(2,1)} fusion(bf16[1024,2560]{1,0:T(8,128)(2,1)S(1)} %bitcast.38, bf16[2560,10240]{1,0:T(8,128)(2,1)} %param.24, f32[10240]{0:T(1024)S(1)} %copy-done.17), kind=kOutput, calls=%fused_computation.clone.clone.clone.1 | convolution fusion | flops 53750005760 | bytes 78684160 | tf_op jit(solution)/shard_map/dot_general | solution.py:289
  884.5 1.4 collective-permute-start.7
  886.0 1.5 copy-done.12
  887.5 62.7 %fusion = f32[1024,2560]{1,0:T(8,128)} fusion(bf16[10240,2560]{1,0:T(8,128)(2,1)} %param.26, bf16[1024,10240]{1,0:T(8,128)(2,1)} %multiply_convert_fusion.clone.4), kind=kOutput, calls=%fused_computation.4 | convolution fusion | flops 53687091200 | bytes 83886080 | tf_op jit(solution)/shard_map/dot_general | solution.py:293
  950.2 49.3 %collective-permute-done.7.rest_6_ = bf16[8,256,640]{2,1,0:T(8,128)(2,1)} collective-permute-done((bf16[8,256,640]{2,1,0:T(8,128)(2,1)S(1)}, bf16[8,256,640]{2,1,0:T(8,128)(2,1)}, u32[]{:S(2)}, u32[]{:S(2)}) %collective-permute-start.7) | collective-permute-done | bytes 2621472 | tf_op jit(solution)/shard_map/ppermute | solution.py:264
  999.5 55.3 %collective-permute-done.8.rest_7_ = bf16[8,256,640]{2,1,0:T(8,128)(2,1)} collective-permute-done((bf16[8,256,640]{2,1,0:T(8,128)(2,1)S(1)}, bf16[8,256,640]{2,1,0:T(8,128)(2,1)}, u32[]{:S(2)}, u32[]{:S(2)}) %collective-permute-start.8) | collective-permute-done | bytes 2621472 | tf_op jit(solution)/shard_map/ppermute | solution.py:264
  1054.8 73.5 %finish.1 = bf16[16,256,2560]{2,1,0:T(8,128)(2,1)} custom-call(s32[1]{0:T(128)} %bitcast.shard_ref, bf16[16,256,2560]{2,1,0:T(8,128)(2,1)} %x_ref.3, f32[1,2560]{1,0:T(1,128)} %broadcast_in_dim.30.b_out_ref, f32[1,2560]{1,0:T(1,128)} %broadcast_in_dim.31.b_down_ref, f32[4,256,2560]{2,1,0:T(8,128)} %bitcast.47, f32[4,256,2560]{2,1,0:T(8,128)} %bitcast.48, ...), custom_call_target="tpu_custom_call" | custom-call | flops 53687091200 | bytes 104857600 | tf_op jit(solution)/shard_map/finish/pallas_call | solution.py:240
  (66 shorter events, 3.1 us)
Async XLA Ops:
  0.6 107.5 %copy-start = (f32[32,3,80]{2,0,1:T(8,128)S(1)}, f32[32,3,80]{2,0,1:T(8,128)}, u32[]{:S(2)}) copy-start(f32[32,3,80]{2,0,1:T(8,128)} %param.21) | copy-start | bytes 92164
  0.6 44.1 %copy-start.16 = (f32[10240]{0:T(1024)S(1)}, f32[10240]{0:T(1024)}, u32[]{:S(2)}) copy-start(f32[10240]{0:T(1024)} %param.25) | copy-start | bytes 122884
  39.8 338.0 %collective-permute-start.4 = (bf16[8,256,2560]{2,1,0:T(8,128)(2,1)}, bf16[8,256,2560]{2,1,0:T(8,128)(2,1)}, u32[]{:S(2)}, u32[]{:S(2)}) collective-permute-start(bf16[8,256,2560]{2,1,0:T(8,128)(2,1)} %get-tuple-element.35.a0), channel_id=1, source_target_pairs={{0,2},{1,3},{2,0},{3,1},{4,6},{5,7},{6,4},{7,5}} | collective-permute-start | bytes 31457288 | tf_op jit(solution)/shard_map/ppermute | solution.py:264
  43.1 450.4 %collective-permute-start.3 = (bf16[8,256,2560]{2,1,0:T(8,128)(2,1)}, bf16[8,256,2560]{2,1,0:T(8,128)(2,1)}, u32[]{:S(2)}, u32[]{:S(2)}) collective-permute-start(bf16[8,256,2560]{2,1,0:T(8,128)(2,1)} %get-tuple-element.35.a0), channel_id=1, source_target_pairs={{0,1},{1,0},{2,3},{3,2},{4,5},{5,4},{6,7},{7,6}} | collective-permute-start | bytes 31457288 | tf_op jit(solution)/shard_map/ppermute | solution.py:264
  43.1 450.4 %collective-permute-start.1 = (bf16[8,256,2560]{2,1,0:T(8,128)(2,1)}, bf16[8,256,2560]{2,1,0:T(8,128)(2,1)}, u32[]{:S(2)}, u32[]{:S(2)}) collective-permute-start(bf16[8,256,2560]{2,1,0:T(8,128)(2,1)} %get-tuple-element.33.a0), channel_id=1, source_target_pairs={{0,2},{1,3},{2,0},{3,1},{4,6},{5,7},{6,4},{7,5}} | collective-permute-start | bytes 31457288 | tf_op jit(solution)/shard_map/ppermute | solution.py:264
  43.1 613.0 %collective-permute-start = (bf16[8,256,2560]{2,1,0:T(8,128)(2,1)}, bf16[8,256,2560]{2,1,0:T(8,128)(2,1)}, u32[]{:S(2)}, u32[]{:S(2)}) collective-permute-start(bf16[8,256,2560]{2,1,0:T(8,128)(2,1)} %get-tuple-element.33.a0), channel_id=1, source_target_pairs={{0,1},{1,0},{2,3},{3,2},{4,5},{5,4},{6,7},{7,6}} | collective-permute-start | bytes 31457288 | tf_op jit(solution)/shard_map/ppermute | solution.py:264
  110.7 76.5 %slice-start = ((s8[5242880]{0:T(1024)(128)(4,1)}), s8[1048576]{0:T(1024)(128)(4,1)S(1)}, s32[]{:S(2)}) async-start(s8[5242880]{0:T(1024)(128)(4,1)} %bitcast.39), calls=%async_computation | async-start | bytes 2097152
  123.2 64.0 %slice-start.1 = ((s8[5242880]{0:T(1024)(128)(4,1)}), s8[4194304]{0:T(1024)(128)(4,1)S(1)}, s32[]{:S(2)}) async-start(s8[5242880]{0:T(1024)(128)(4,1)} %bitcast.39), calls=%async_computation.1 | async-start | bytes 8388608
  187.2 61.9 %copy-start.3 = (f32[2560]{0:T(1024)S(1)}, f32[2560]{0:T(1024)}, u32[]{:S(2)}) copy-start(f32[2560]{0:T(1024)} %param.23) | copy-start | bytes 30724
  187.2 62.5 %copy-start.4 = (f32[2560]{0:T(1024)S(1)}, f32[2560]{0:T(1024)}, u32[]{:S(2)}) copy-start(f32[2560]{0:T(1024)} %param.27) | copy-start | bytes 30724
  187.2 63.8 %copy-start.2 = (f32[1024]{0:T(1024)S(1)}, f32[1024]{0:T(1024)}, u32[]{:S(2)}) copy-start(f32[1024]{0:T(1024)} %iota_convert_fusion) | copy-start | bytes 12292
  187.2 63.8 %copy-start.5 = (f32[10]{0:T(128)S(1)}, f32[10]{0:T(128)}, u32[]{:S(2)}) copy-start(f32[10]{0:T(128)} %multiply_power_fusion) | copy-start | bytes 124
  251.3 62.9 %copy-start.6 = (f32[24]{0:T(128)S(1)}, f32[24]{0:T(128)}, u32[]{:S(2)}) copy-start(f32[24]{0:T(128)} %pad.10.clone) | copy-start | bytes 292
  251.3 62.9 %copy-start.7 = (f32[24]{0:T(128)S(1)}, f32[24]{0:T(128)}, u32[]{:S(2)}) copy-start(f32[24]{0:T(128)} %pad.7.clone) | copy-start | bytes 292
  377.8 115.7 %collective-permute-start.5 = (bf16[8,256,2560]{2,1,0:T(8,128)(2,1)}, bf16[8,256,2560]{2,1,0:T(8,128)(2,1)}, u32[]{:S(2)}, u32[]{:S(2)}) collective-permute-start(bf16[8,256,2560]{2,1,0:T(8,128)(2,1)} %collective-permute-done.4.a2), channel_id=1, source_target_pairs={{0,1},{1,0},{2,3},{3,2},{4,5},{5,4},{6,7},{7,6}} | collective-permute-start | bytes 31457288 | tf_op jit(solution)/shard_map/ppermute | solution.py:264
  493.5 162.7 %collective-permute-start.2 = (bf16[8,256,2560]{2,1,0:T(8,128)(2,1)}, bf16[8,256,2560]{2,1,0:T(8,128)(2,1)}, u32[]{:S(2)}, u32[]{:S(2)}) collective-permute-start(bf16[8,256,2560]{2,1,0:T(8,128)(2,1)} %collective-permute-done.1.a2), channel_id=1, source_target_pairs={{0,1},{1,0},{2,3},{3,2},{4,5},{5,4},{6,7},{7,6}} | collective-permute-start | bytes 31457288 | tf_op jit(solution)/shard_map/ppermute | solution.py:264
  656.2 165.2 %copy-start.8 = (bf16[4,256,2560]{2,1,0:T(8,128)(2,1)S(1)}, bf16[4,256,2560]{2,1,0:T(8,128)(2,1)}, u32[]{:S(2)}) copy-start(bf16[4,256,2560]{2,1,0:T(8,128)(2,1)} %get-tuple-element.42) | copy-start | bytes 15728644
  656.2 165.2 %copy-start.17 = (f32[10240]{0:T(1024)S(1)}, f32[10240]{0:T(1024)}, u32[]{:S(2)}) copy-start(f32[10240]{0:T(1024)} %param.25) | copy-start | bytes 122884
  819.7 66.3 %collective-permute-start.10 = (bf16[8,256,640]{2,1,0:T(8,128)(2,1)}, bf16[8,256,640]{2,1,0:T(8,128)(2,1)S(1)}, u32[]{:S(2)}, u32[]{:S(2)}) collective-permute-start(bf16[8,256,640]{2,1,0:T(8,128)(2,1)} %get-tuple-element.49), channel_id=1, source_target_pairs={{0,2},{1,3},{2,0},{3,1},{4,6},{5,7},{6,4},{7,5}} | collective-permute-start | bytes 7864328 | tf_op jit(solution)/shard_map/ppermute | solution.py:264
  821.4 62.2 %copy-start.15 = (bf16[8,256,640]{2,1,0:T(8,128)(2,1)S(1)}, bf16[8,256,640]{2,1,0:T(8,128)(2,1)}, u32[]{:S(2)}) copy-start(bf16[8,256,640]{2,1,0:T(8,128)(2,1)} %get-tuple-element.50) | copy-start | bytes 7864324
  821.4 62.6 %copy-start.13 = (bf16[8,256,640]{2,1,0:T(8,128)(2,1)S(1)}, bf16[8,256,640]{2,1,0:T(8,128)(2,1)}, u32[]{:S(2)}) copy-start(bf16[8,256,640]{2,1,0:T(8,128)(2,1)} %get-tuple-element.48) | copy-start | bytes 7864324
  821.4 62.7 %copy-start.11 = (bf16[8,256,640]{2,1,0:T(8,128)(2,1)S(1)}, bf16[8,256,640]{2,1,0:T(8,128)(2,1)}, u32[]{:S(2)}) copy-start(bf16[8,256,640]{2,1,0:T(8,128)(2,1)} %get-tuple-element.44) | copy-start | bytes 7864324
  821.4 63.1 %copy-start.10 = (bf16[8,256,640]{2,1,0:T(8,128)(2,1)S(1)}, bf16[8,256,640]{2,1,0:T(8,128)(2,1)}, u32[]{:S(2)}) copy-start(bf16[8,256,640]{2,1,0:T(8,128)(2,1)} %get-tuple-element.45) | copy-start | bytes 7864324
  821.4 66.1 %copy-start.9 = (bf16[8,256,640]{2,1,0:T(8,128)(2,1)S(1)}, bf16[8,256,640]{2,1,0:T(8,128)(2,1)}, u32[]{:S(2)}) copy-start(bf16[8,256,640]{2,1,0:T(8,128)(2,1)} %get-tuple-element.46) | copy-start | bytes 7864324
  883.6 66.5 %collective-permute-start.11 = (bf16[8,256,640]{2,1,0:T(8,128)(2,1)S(1)}, bf16[8,256,640]{2,1,0:T(8,128)(2,1)S(1)}, u32[]{:S(2)}, u32[]{:S(2)}) collective-permute-start(bf16[8,256,640]{2,1,0:T(8,128)(2,1)S(1)} %copy-done.15), channel_id=1, source_target_pairs={{0,3},{1,2},{2,1},{3,0},{4,7},{5,6},{6,5},{7,4}} | collective-permute-start | bytes 7864328 | tf_op jit(solution)/shard_map/ppermute | solution.py:264
  884.0 66.1 %collective-permute-start.9 = (bf16[8,256,640]{2,1,0:T(8,128)(2,1)S(1)}, bf16[8,256,640]{2,1,0:T(8,128)(2,1)}, u32[]{:S(2)}, u32[]{:S(2)}) collective-permute-start(bf16[8,256,640]{2,1,0:T(8,128)(2,1)S(1)} %copy-done.13), channel_id=1, source_target_pairs={{0,1},{1,0},{2,3},{3,2},{4,5},{5,4},{6,7},{7,6}} | collective-permute-start | bytes 7864328 | tf_op jit(solution)/shard_map/ppermute | solution.py:264
  884.1 66.1 %collective-permute-start.6 = (bf16[8,256,640]{2,1,0:T(8,128)(2,1)S(1)}, bf16[8,256,640]{2,1,0:T(8,128)(2,1)}, u32[]{:S(2)}, u32[]{:S(2)}) collective-permute-start(bf16[8,256,640]{2,1,0:T(8,128)(2,1)S(1)} %copy-done.11), channel_id=1, source_target_pairs={{0,1},{1,0},{2,3},{3,2},{4,5},{5,4},{6,7},{7,6}} | collective-permute-start | bytes 7864328 | tf_op jit(solution)/shard_map/ppermute | solution.py:264
  884.5 114.9 %collective-permute-start.7 = (bf16[8,256,640]{2,1,0:T(8,128)(2,1)S(1)}, bf16[8,256,640]{2,1,0:T(8,128)(2,1)}, u32[]{:S(2)}, u32[]{:S(2)}) collective-permute-start(bf16[8,256,640]{2,1,0:T(8,128)(2,1)S(1)} %copy-done.10), channel_id=1, source_target_pairs={{0,2},{1,3},{2,0},{3,1},{4,6},{5,7},{6,4},{7,5}} | collective-permute-start | bytes 7864328 | tf_op jit(solution)/shard_map/ppermute | solution.py:264
  886.0 1.5 copy-start.12
  887.5 167.3 %collective-permute-start.8 = (bf16[8,256,640]{2,1,0:T(8,128)(2,1)S(1)}, bf16[8,256,640]{2,1,0:T(8,128)(2,1)}, u32[]{:S(2)}, u32[]{:S(2)}) collective-permute-start(bf16[8,256,640]{2,1,0:T(8,128)(2,1)S(1)} %copy-done.9), channel_id=1, source_target_pairs={{0,3},{1,2},{2,1},{3,0},{4,7},{5,6},{6,5},{7,4}} | collective-permute-start | bytes 7864328 | tf_op jit(solution)/shard_map/ppermute | solution.py:264
  950.2 104.7 %copy-start.14 = (bf16[8,256,640]{2,1,0:T(8,128)(2,1)}, bf16[8,256,640]{2,1,0:T(8,128)(2,1)S(1)}, u32[]{:S(2)}) copy-start(bf16[8,256,640]{2,1,0:T(8,128)(2,1)S(1)} %collective-permute-done.11.rest_11_) | copy-start | bytes 7864324
  1054.8 73.5 %copy-start.1 = (f32[32,3,80]{2,0,1:T(8,128)S(1)}, f32[32,3,80]{2,0,1:T(8,128)}, u32[]{:S(2)}) copy-start(f32[32,3,80]{2,0,1:T(8,128)} %param.21) | copy-start | bytes 92164
